TPU v7x, 32 devices: a whole 2x2x4 slice. The times are simulated.
32 devices in a mesh: beam: 2 (over x), chan: 16 (over z, y, core).
Axes of the slice: x: 2, y: 2, z: 4, core: 2. Of those that a mesh axis runs over, the one named last changes fastest.
Arguments:
- spectra: float32 [4096, 1024], P(('beam', 'chan')), parts along dimension 0, may hold values from -6 to 6
- chan_delay: int32 [2048, 32], P('chan'), may hold values from 0 to 63
- window_base: int32 [16, 64], P(None, 'chan'), may hold values from 0 to 28
- trial_offset: int32 [256, 64], P('chan'), may hold values from 0 to 3
- shift_blocks: int32 [256], P('chan'), may hold values from 0 to 7
- template_len: int32 [8], replicated, may hold values from 1 to 128
Outputs:
- scores: float32 [512, 8, 1024], P(('beam', 'chan')), parts along dimension 0
There are 2 independent parts, one for each index of `beam`. A program takes and returns all parts, laid end to end along the dimension named above; an argument that names none is the same for every part. Nothing has to cross between parts.
All inputs are finite; a program needn't handle non-finite values.
Results may differ from a plain program's by a relative error of at most 0.0032.
Values may be sent and summed in bfloat16 or wider, within the bound.
No kernel may reach another device: no remote copies, remote signals or barrier semaphores. Data moves between devices by JAX's collectives and lax.ppermute only.
A program may use at most 64 MiB of HBM per device.

v0:
```python
import functools

import jax
import jax.numpy as jnp
from jax import lax
from jax.experimental import pallas as pl
from jax.experimental.pallas import tpu as pltpu
from jax.sharding import PartitionSpec as P


SUB_CH = 32
NDELAY = 32
MAXD = 64
SPAN = 4
BLOCK = 128
FINE = 8
COARSE = MAXD // FINE
TILE = 256
HALF = 16
CORES = 2
ORDER = (4, 5, 3, 6, 7, 2, 1)


def later(x, amount):
    if amount == 0:
        return x
    moved = pltpu.roll(x, amount, 1)
    lane = lax.broadcasted_iota(jnp.int32, (x.shape[0], BLOCK), 1)
    first = jnp.where(lane >= amount, moved[:, :BLOCK], jnp.zeros((), x.dtype))
    return jnp.concatenate([first, moved[:, BLOCK:]], axis=1)


def partner(chip, distance):
    return chip ^ distance


def column(row, size):
    same = lax.broadcasted_iota(jnp.int32, (size, size), 0) == lax.broadcasted_iota(jnp.int32, (size, size), 1)
    return jnp.sum(jnp.where(same, row.astype(jnp.float32), 0.0), axis=1, keepdims=True).astype(jnp.int32)


def rows_kernel(
    spectra_hbm, delay_hbm, base_hbm, keep_ref, give_ref,
    spectra_ref, delay_ref, base_ref, tables_ref, terms_ref, sums_ref, rows_ref, sems,
):
    me = lax.axis_index("chan")
    chip, core = me // CORES, me % CORES
    channels, samples = spectra_ref.shape
    bands = channels // SUB_CH
    owners = base_ref.shape[1]
    depth = FINE * SUB_CH
    count = bands * SPAN
    chips = owners // CORES
    blocks = samples // BLOCK

    large = []
    for band in range(bands):
        part = pl.ds(band * SUB_CH, SUB_CH)
        large.append(pltpu.make_async_copy(spectra_hbm.at[part], spectra_ref.at[part], sems.at[band]))
    delays = pltpu.make_async_copy(delay_hbm, delay_ref, sems.at[bands])
    bases = pltpu.make_async_copy(base_hbm, base_ref, sems.at[bands + 1])
    large[0].start()
    delays.start()
    for copy in large[1:]:
        copy.start()
    bases.start()
    rows_ref[:, bands * NDELAY :, :] = jnp.zeros((blocks, rows_ref.shape[1] - bands * NDELAY, BLOCK), jnp.float32)

    def tabulate(band):
        lane = lax.broadcasted_iota(jnp.int32, (NDELAY, channels), 1)
        tiled = jnp.where(lane // SUB_CH == band, delay_ref[...], 0)
        step = SUB_CH
        while step < channels:
            tiled = tiled + pltpu.roll(tiled, step, 1)
            step *= 2
        for coarse in range(COARSE):
            for start in range(0, FINE, bands):
                wanted = coarse * FINE + start + lane // SUB_CH
                table = jnp.where(tiled == wanted, 1.0, 0.0).astype(jnp.bfloat16)
                tables_ref[band, coarse * NDELAY : (coarse + 1) * NDELAY, start * SUB_CH : start * SUB_CH + channels] = table

    def fill(band, fine):
        slot = band % 2
        for start in range(0, SUB_CH, HALF):
            at = fine * SUB_CH + start
            if fine == 0:
                first = spectra_ref[band * SUB_CH + start : band * SUB_CH + start + HALF, :]
                high = first.astype(jnp.bfloat16)
                low = (first - high.astype(jnp.float32)).astype(jnp.bfloat16)
            else:
                high = later(terms_ref[slot, start : start + HALF, :], fine)
                low = later(terms_ref[slot, depth + start : depth + start + HALF, :], fine)
            terms_ref[slot, at : at + HALF, :] = high
            terms_ref[slot, depth + at : depth + at + HALF, :] = low

    def multiply(band, tile):
        slot = band % 2
        table = tables_ref[band]
        both = jnp.concatenate([table, table], axis=1)
        columns = slice(tile * TILE, (tile + 1) * TILE)
        sums_ref[slot, :, columns] = jnp.dot(both, terms_ref[slot, :, columns], preferred_element_type=jnp.float32)

    def drain(band, start):
        slot = band % 2
        total = sums_ref[slot, start : start + HALF, :]
        for coarse in range(1, COARSE):
            at = coarse * NDELAY + start
            total = total + later(sums_ref[slot, at : at + HALF, :], coarse * FINE)
        total = total * SUB_CH ** (-0.5)
        for block in range(blocks):
            at = band * NDELAY + start
            rows_ref[block, at : at + HALF, :] = total[:, block * BLOCK : (block + 1) * BLOCK]

    tiles = samples // TILE
    for step in range(bands + 2):
        if step < bands:
            large[step].wait()
        for tile in range(tiles):
            if step < bands:
                for fine in range(tile * FINE // tiles, (tile + 1) * FINE // tiles):
                    fill(step, fine)
            if 1 <= step <= bands:
                multiply(step - 1, tile)
            if step >= 2:
                for start in range(0, NDELAY, HALF):
                    if (start // HALF + 1) * tiles // (NDELAY // HALF) - 1 == tile:
                        drain(step - 2, start)
        if step < bands:
            if step == 0:
                delays.wait()
            tabulate(step)

    bases.wait()
    place = lax.broadcasted_iota(jnp.int32, (2 * SPAN, BLOCK), 0)
    for side, target in ((1, give_ref), (0, keep_ref)):
        for distance in range(chips):
            owner = partner(chip, distance) * CORES + (core + side) % CORES
            begins = [band * NDELAY + base_ref[band, owner] for band in range(bands)]
            for block in range(blocks):
                pairs = []
                for band in range(0, bands, 2):
                    upper = rows_ref[block, pl.ds(begins[band], 2 * SPAN), :]
                    lower = rows_ref[block, pl.ds(begins[band + 1] - SPAN, 2 * SPAN), :]
                    pairs.append(jnp.where(place < SPAN, upper, lower))
                picked = jnp.concatenate(pairs, axis=0).astype(jnp.bfloat16)
                target[distance * count : (distance + 1) * count, block * BLOCK : (block + 1) * BLOCK] = picked


def tables_kernel(offset_ref, shift_in, length_in, picker_ref, shift_ref, length_ref, ones_ref, *, bands):
    me = lax.axis_index("chan")
    chip, core = me // CORES, me % CORES
    subbands = offset_ref.shape[1]
    place = lax.broadcasted_iota(jnp.int32, (subbands, subbands * SPAN), 1) // SPAN
    side = place // bands % CORES
    spread = (partner(chip, place // (bands * CORES)) * CORES + (core + side) % CORES) * bands + place % bands
    spread = (spread == lax.broadcasted_iota(jnp.int32, (subbands, subbands * SPAN), 0)).astype(jnp.bfloat16)
    wide = jnp.dot(offset_ref[...].astype(jnp.bfloat16), spread, preferred_element_type=jnp.float32)
    span_of = (lax.broadcasted_iota(jnp.int32, wide.shape, 1) % SPAN).astype(jnp.float32)
    picker_ref[...] = jnp.where(wide == span_of, 1.0, 0.0).astype(jnp.bfloat16)
    shift_ref[...] = jnp.broadcast_to(column(shift_in[...], shift_ref.shape[0]), shift_ref.shape)
    length_ref[...] = jnp.broadcast_to(column(length_in[...], length_ref.shape[0]), length_ref.shape)
    row = lax.broadcasted_iota(jnp.int32, ones_ref.shape, 0) % BLOCK
    lane = lax.broadcasted_iota(jnp.int32, ones_ref.shape, 1)
    ones_ref[...] = jnp.where((row < lane) | (lane >= BLOCK), 1.0, 0.0).astype(jnp.bfloat16)


def join_kernel(keep_ref, got_ref, *parts):
    count = parts[0].shape[0] // CORES
    for distance, part in zip(order(len(parts) + 1), parts):
        rows = slice(distance * count, (distance + 1) * count)
        part[:count, :] = keep_ref[rows, :]
        part[count:, :] = got_ref[rows, :]


def scores_kernel(keep_ref, got_ref, picker_ref, shift_ref, length_ref, ones_ref, *rest):
    *parts, out_hbm, prefix_ref, after_ref, out_ref, sems = rest
    trials, templates, samples = out_ref.shape
    blocks = samples // BLOCK
    subbands = picker_ref.shape[1] // SPAN
    count = parts[0].shape[0] // CORES
    near = dict(zip(order(len(parts) + 1), parts))
    stacked = [keep_ref[:count, :], got_ref[:count, :]] + [near[distance][...] for distance in sorted(near)]
    stacked = jnp.concatenate(stacked, axis=0)
    summed = jnp.dot(picker_ref[...], stacked, preferred_element_type=jnp.float32) * subbands ** (-0.5)
    current = [summed[:, b * BLOCK : (b + 1) * BLOCK] for b in range(blocks)]
    shift = shift_ref[...]
    bit = 1
    while bit < blocks:
        taken = (shift & bit) != 0
        current = [jnp.where(taken, current[b + bit] if b + bit < blocks else 0.0, current[b]) for b in range(blocks)]
        bit *= 2
    whole = jnp.concatenate(current, axis=0)
    high = whole.astype(jnp.bfloat16)
    rest = whole - high.astype(jnp.float32)
    middle = rest.astype(jnp.bfloat16)
    low = (rest - middle.astype(jnp.float32)).astype(jnp.bfloat16)
    both = jnp.dot(jnp.concatenate([high, middle, low], axis=1), ones_ref[...], preferred_element_type=jnp.float32)
    for b in range(blocks):
        columns = slice(b * BLOCK, (b + 1) * BLOCK)
        prefix_ref[:, columns] = both[b * trials : (b + 1) * trials, :BLOCK]
        after = both[b * trials : (b + 1) * trials, BLOCK:]
        if b + 1 < blocks:
            after = after + both[(b + 1) * trials : (b + 2) * trials, :BLOCK]
        after_ref[:, columns] = after
    length = length_ref[...]
    lane = lax.broadcasted_iota(jnp.int32, (templates, BLOCK), 1)
    source = (lane + length) % BLOCK
    from_next = lane < length
    weight = lax.rsqrt(length.astype(jnp.float32))
    chunk = trials // sems.shape[0]
    copies = []
    for j in range(trials):
        for b in range(blocks):
            columns = slice(b * BLOCK, (b + 1) * BLOCK)
            here = jnp.broadcast_to(prefix_ref[j : j + 1, columns], (templates, BLOCK))
            there = jnp.broadcast_to(after_ref[j : j + 1, columns], (templates, BLOCK))
            ends = jnp.take_along_axis(jnp.where(from_next, there, here), source, axis=1)
            out_ref[j, :, columns] = (ends - here) * weight
        if (j + 1) % chunk == 0:
            part = pl.ds(j + 1 - chunk, chunk)
            copies.append(pltpu.make_async_copy(out_ref.at[part], out_hbm.at[part], sems.at[len(copies)]))
            copies[-1].start()
    for copy in copies:
        copy.wait()


def order(chips):
    if chips == len(ORDER) + 1:
        return ORDER
    return tuple(range(1, chips))


def local(spectra, chan_delay, window_base, trial_offset, shift_blocks, template_len):
    channels, samples = spectra.shape
    owners = window_base.shape[0]
    bands = channels // SUB_CH
    trials, subbands = trial_offset.shape
    templates = template_len.shape[0]
    count = bands * SPAN
    chips = owners // CORES
    depth = FINE * SUB_CH
    anywhere = pl.BlockSpec(memory_space=pltpu.HBM)
    inside = pl.BlockSpec(memory_space=pltpu.VMEM)
    limits = pltpu.CompilerParams(vmem_limit_bytes=24 * 1024 * 1024)
    arrays = [
        pltpu.with_memory_space_constraint(array, pltpu.HBM)
        for array in (spectra, chan_delay.T, window_base.T, trial_offset, shift_blocks.reshape(1, trials), template_len.reshape(1, templates))
    ]
    keep, give = pl.pallas_call(
        rows_kernel,
        out_shape=[pltpu.VMEM((chips * count, samples), jnp.bfloat16)] * 2,
        in_specs=[anywhere] * 3,
        scratch_shapes=[
            pltpu.VMEM((channels, samples), jnp.float32),
            pltpu.VMEM((NDELAY, channels), jnp.int32),
            pltpu.SMEM((bands, owners), jnp.int32),
            pltpu.VMEM((bands, COARSE * NDELAY, depth), jnp.bfloat16),
            pltpu.VMEM((2, 2 * depth, samples), jnp.bfloat16),
            pltpu.VMEM((2, COARSE * NDELAY, samples), jnp.float32),
            pltpu.VMEM((samples // BLOCK, bands * NDELAY + 2 * SPAN, BLOCK), jnp.float32),
            pltpu.SemaphoreType.DMA((bands + 2,)),
        ],
        compiler_params=limits,
        name="rows",
    )(*arrays[:3])
    picker, shift, length, ones = pl.pallas_call(
        functools.partial(tables_kernel, bands=bands),
        out_shape=(
            pltpu.VMEM((trials, subbands * SPAN), jnp.bfloat16),
            pltpu.VMEM((trials, BLOCK), jnp.int32),
            pltpu.VMEM((templates, BLOCK), jnp.int32),
            pltpu.VMEM((3 * BLOCK, 2 * BLOCK), jnp.bfloat16),
        ),
        compiler_params=limits,
        name="tables",
    )(*arrays[3:])
    devices = range(owners)
    got = lax.ppermute(give, "chan", [(i, i ^ 1) for i in devices])
    got = pltpu.with_memory_space_constraint(got, pltpu.VMEM)
    parts = pl.pallas_call(
        join_kernel,
        out_shape=[pltpu.VMEM((CORES * count, samples), jnp.bfloat16)] * (chips - 1),
        in_specs=[inside] * 2,
        compiler_params=limits,
        name="join",
    )(keep, got)
    arrived = []
    for distance, part in zip(order(chips), parts):
        part = lax.ppermute(part, "chan", [(i, partner(i // CORES, distance) * CORES + i % CORES) for i in devices])
        arrived.append(pltpu.with_memory_space_constraint(part, pltpu.VMEM))
    return pl.pallas_call(
        scores_kernel,
        out_shape=jax.ShapeDtypeStruct((trials, templates, samples), jnp.float32),
        in_specs=[inside] * (6 + len(arrived)),
        out_specs=anywhere,
        scratch_shapes=[
            pltpu.VMEM((trials, samples), jnp.float32),
            pltpu.VMEM((trials, samples), jnp.float32),
            pltpu.VMEM((trials, templates, samples), jnp.float32),
            pltpu.SemaphoreType.DMA((4,)),
        ],
        compiler_params=limits,
        name="scores",
    )(keep, got, picker, shift, length, ones, *arrived)


def solution(mesh):
    in_specs = (
        P(("beam", "chan"), None),
        P("chan", None),
        P(None, "chan"),
        P("chan", None),
        P("chan"),
        P(),
    )
    out_specs = P(("beam", "chan"), None, None)

    return jax.shard_map(local, mesh=mesh, in_specs=in_specs, out_specs=out_specs, check_vma=False)
```

profile of v0, /device:TPU:0, one launch (start us, length us, event | category | flops | bytes accessed | tf_op | source)
XLA Modules:
  0.0 24.3 jit_solution(12133403382534726190)
XLA Ops:
  0.0 4.1 %rows.1 = (bf16[128,1024]{1,0:T(8,128)(2,1)S(1)}, bf16[128,1024]{1,0:T(8,128)(2,1)S(1)}) custom-call(f32[128,1024]{1,0:T(8,128)} %spectra_hbm.1, s32[32,128]{1,0:T(8,128)} %bitcast.4, s32[4,16]{1,0:T(4,128)} %bitcast.5), custom_call_target="tpu_custom_call" | custom-call | tf_op jit(solution)/shard_map/rows/pallas_call | solution.py:249
  4.1 0.6 %collective-permute-start = (bf16[128,1024]{1,0:T(8,128)(2,1)S(1)}, bf16[128,1024]{1,0:T(8,128)(2,1)S(1)}, u32[]{:S(2)}, u32[]{:S(2)}) collective-permute-start(bf16[128,1024]{1,0:T(8,128)(2,1)S(1)} %get-tuple-element.19), channel_id=1, source_target_pairs={{0,1},{1,0},{2,3},{3,2},{4,5},{5,4},{6,7},{7,6},{8,9},{9,8},{10,11... | collective-permute-start | bytes 786440 | tf_op jit(solution)/shard_map/ppermute | solution.py:278
  4.6 1.2 %collective-permute-done.got_ref = bf16[128,1024]{1,0:T(8,128)(2,1)S(1)} collective-permute-done((bf16[128,1024]{1,0:T(8,128)(2,1)S(1)}, bf16[128,1024]{1,0:T(8,128)(2,1)S(1)}, u32[]{:S(2)}, u32[]{:S(2)}) %collective-permute-start) | collective-permute-done | bytes 262176 | tf_op jit(solution)/shard_map/ppermute | solution.py:278
  5.8 4.0 %collective-permute-start.1 = (bf16[32,1024]{1,0:T(8,128)(2,1)S(1)}, bf16[32,1024]{1,0:T(8,128)(2,1)S(1)}, u32[]{:S(2)}, u32[]{:S(2)}) collective-permute-start(bf16[32,1024]{1,0:T(8,128)(2,1)S(1)} %get-tuple-element.24), channel_id=1, source_target_pairs={{0,8},{1,9},{2,10},{3,11},{4,12},{5,13},{6,14},{7,15},{8,0},{9,1},... | collective-permute-start | bytes 196616 | tf_op jit(solution)/shard_map/ppermute | solution.py:289
  9.8 1.3 %collective-permute-start.2 = (bf16[32,1024]{1,0:T(8,128)(2,1)S(1)}, bf16[32,1024]{1,0:T(8,128)(2,1)S(1)}, u32[]{:S(2)}, u32[]{:S(2)}) collective-permute-start(bf16[32,1024]{1,0:T(8,128)(2,1)S(1)} %get-tuple-element.25), channel_id=1, source_target_pairs={{0,10},{1,11},{2,8},{3,9},{4,14},{5,15},{6,12},{7,13},{8,2},{9,3},... | collective-permute-start | bytes 196616 | tf_op jit(solution)/shard_map/ppermute | solution.py:289
  11.1 1.5 %collective-permute-start.3 = (bf16[32,1024]{1,0:T(8,128)(2,1)S(1)}, bf16[32,1024]{1,0:T(8,128)(2,1)S(1)}, u32[]{:S(2)}, u32[]{:S(2)}) collective-permute-start(bf16[32,1024]{1,0:T(8,128)(2,1)S(1)} %get-tuple-element.26), channel_id=1, source_target_pairs={{0,6},{1,7},{2,4},{3,5},{4,2},{5,3},{6,0},{7,1},{8,14},{9,15},{10,... | collective-permute-start | bytes 196616 | tf_op jit(solution)/shard_map/ppermute | solution.py:289
  12.7 2.5 %collective-permute-start.4 = (bf16[32,1024]{1,0:T(8,128)(2,1)S(1)}, bf16[32,1024]{1,0:T(8,128)(2,1)S(1)}, u32[]{:S(2)}, u32[]{:S(2)}) collective-permute-start(bf16[32,1024]{1,0:T(8,128)(2,1)S(1)} %get-tuple-element.27), channel_id=1, source_target_pairs={{0,12},{1,13},{2,14},{3,15},{4,8},{5,9},{6,10},{7,11},{8,4},{9,5},... | collective-permute-start | bytes 196616 | tf_op jit(solution)/shard_map/ppermute | solution.py:289
  15.1 2.3 %collective-permute-start.5 = (bf16[32,1024]{1,0:T(8,128)(2,1)S(1)}, bf16[32,1024]{1,0:T(8,128)(2,1)S(1)}, u32[]{:S(2)}, u32[]{:S(2)}) collective-permute-start(bf16[32,1024]{1,0:T(8,128)(2,1)S(1)} %get-tuple-element.28), channel_id=1, source_target_pairs={{0,14},{1,15},{2,12},{3,13},{4,10},{5,11},{6,8},{7,9},{8,6},{9,7},... | collective-permute-start | bytes 196616 | tf_op jit(solution)/shard_map/ppermute | solution.py:289
  17.4 0.0 collective-permute-done.1.rest_0_
  17.4 0.0 collective-permute-start.6
  17.4 0.9 %collective-permute-done.2.rest_1_ = bf16[32,1024]{1,0:T(8,128)(2,1)S(1)} collective-permute-done((bf16[32,1024]{1,0:T(8,128)(2,1)S(1)}, bf16[32,1024]{1,0:T(8,128)(2,1)S(1)}, u32[]{:S(2)}, u32[]{:S(2)}) %collective-permute-start.2) | collective-permute-done | bytes 65568 | tf_op jit(solution)/shard_map/ppermute | solution.py:289
  18.4 1.8 %collective-permute-start.7 = (bf16[32,1024]{1,0:T(8,128)(2,1)S(1)}, bf16[32,1024]{1,0:T(8,128)(2,1)S(1)}, u32[]{:S(2)}, u32[]{:S(2)}) collective-permute-start(bf16[32,1024]{1,0:T(8,128)(2,1)S(1)} %get-tuple-element.30), channel_id=1, source_target_pairs={{0,2},{1,3},{2,0},{3,1},{4,6},{5,7},{6,4},{7,5},{8,10},{9,11},{10,... | collective-permute-start | bytes 196616 | tf_op jit(solution)/shard_map/ppermute | solution.py:289
  20.1 0.9 %tables.1 = (bf16[16,256]{1,0:T(8,128)(2,1)S(1)}, s32[16,128]{1,0:T(8,128)S(1)}, s32[8,128]{1,0:T(8,128)S(1)}, bf16[384,256]{1,0:T(8,128)(2,1)S(1)}) custom-call(s32[16,64]{1,0:T(8,128)} %offset_ref.1, s32[1,16]{1,0:T(1,128)} %bitcast.6, s32[1,8]{1,0:T(1,128)} %bitcast.7), custom_call_target="tpu_custom_call" | custom-call | tf_op jit(solution)/shard_map/tables/pallas_call | solution.py:266
  21.0 0.0 collective-permute-done.3.rest_2_
  21.0 0.0 collective-permute-done.4.rest_3_
  21.0 1.2 %collective-permute-done.5.rest_4_ = bf16[32,1024]{1,0:T(8,128)(2,1)S(1)} collective-permute-done((bf16[32,1024]{1,0:T(8,128)(2,1)S(1)}, bf16[32,1024]{1,0:T(8,128)(2,1)S(1)}, u32[]{:S(2)}, u32[]{:S(2)}) %collective-permute-start.5) | collective-permute-done | bytes 65568 | tf_op jit(solution)/shard_map/ppermute | solution.py:289
  22.2 0.2 collective-permute-done.6.rest_5_
  22.4 0.5 %collective-permute-done.7.rest_6_ = bf16[32,1024]{1,0:T(8,128)(2,1)S(1)} collective-permute-done((bf16[32,1024]{1,0:T(8,128)(2,1)S(1)}, bf16[32,1024]{1,0:T(8,128)(2,1)S(1)}, u32[]{:S(2)}, u32[]{:S(2)}) %collective-permute-start.7) | collective-permute-done | bytes 65568 | tf_op jit(solution)/shard_map/ppermute | solution.py:289
  22.9 1.4 %scores.1 = f32[16,8,1024]{2,1,0:T(8,128)} custom-call(bf16[128,1024]{1,0:T(8,128)(2,1)S(1)} %get-tuple-element.18.keep_ref, bf16[128,1024]{1,0:T(8,128)(2,1)S(1)} %collective-permute-done.got_ref, bf16[16,256]{1,0:T(8,128)(2,1)S(1)} %get-tuple-element.20.picker_ref, s32[16,128]{1,0:T(8,128)S(1)} %get-tuple-element.21.shift_ref, ...), custom_call_target="tpu_custom_call" | custom-call | tf_op jit(solution)/shard_map/scores/pallas_call | solution.py:291
  (1 shorter events, 0.0 us)
Async XLA Ops:
  4.1 1.7 %collective-permute-start = (bf16[128,1024]{1,0:T(8,128)(2,1)S(1)}, bf16[128,1024]{1,0:T(8,128)(2,1)S(1)}, u32[]{:S(2)}, u32[]{:S(2)}) collective-permute-start(bf16[128,1024]{1,0:T(8,128)(2,1)S(1)} %get-tuple-element.19), channel_id=1, source_target_pairs={{0,1},{1,0},{2,3},{3,2},{4,5},{5,4},{6,7},{7,6},{8,9},{9,8},{10,11... | collective-permute-start | bytes 786440 | tf_op jit(solution)/shard_map/ppermute | solution.py:278
  5.8 11.6 %collective-permute-start.1 = (bf16[32,1024]{1,0:T(8,128)(2,1)S(1)}, bf16[32,1024]{1,0:T(8,128)(2,1)S(1)}, u32[]{:S(2)}, u32[]{:S(2)}) collective-permute-start(bf16[32,1024]{1,0:T(8,128)(2,1)S(1)} %get-tuple-element.24), channel_id=1, source_target_pairs={{0,8},{1,9},{2,10},{3,11},{4,12},{5,13},{6,14},{7,15},{8,0},{9,1},... | collective-permute-start | bytes 196616 | tf_op jit(solution)/shard_map/ppermute | solution.py:289
  9.8 8.5 %collective-permute-start.2 = (bf16[32,1024]{1,0:T(8,128)(2,1)S(1)}, bf16[32,1024]{1,0:T(8,128)(2,1)S(1)}, u32[]{:S(2)}, u32[]{:S(2)}) collective-permute-start(bf16[32,1024]{1,0:T(8,128)(2,1)S(1)} %get-tuple-element.25), channel_id=1, source_target_pairs={{0,10},{1,11},{2,8},{3,9},{4,14},{5,15},{6,12},{7,13},{8,2},{9,3},... | collective-permute-start | bytes 196616 | tf_op jit(solution)/shard_map/ppermute | solution.py:289
  11.1 9.9 %collective-permute-start.3 = (bf16[32,1024]{1,0:T(8,128)(2,1)S(1)}, bf16[32,1024]{1,0:T(8,128)(2,1)S(1)}, u32[]{:S(2)}, u32[]{:S(2)}) collective-permute-start(bf16[32,1024]{1,0:T(8,128)(2,1)S(1)} %get-tuple-element.26), channel_id=1, source_target_pairs={{0,6},{1,7},{2,4},{3,5},{4,2},{5,3},{6,0},{7,1},{8,14},{9,15},{10,... | collective-permute-start | bytes 196616 | tf_op jit(solution)/shard_map/ppermute | solution.py:289
  12.7 8.4 %collective-permute-start.4 = (bf16[32,1024]{1,0:T(8,128)(2,1)S(1)}, bf16[32,1024]{1,0:T(8,128)(2,1)S(1)}, u32[]{:S(2)}, u32[]{:S(2)}) collective-permute-start(bf16[32,1024]{1,0:T(8,128)(2,1)S(1)} %get-tuple-element.27), channel_id=1, source_target_pairs={{0,12},{1,13},{2,14},{3,15},{4,8},{5,9},{6,10},{7,11},{8,4},{9,5},... | collective-permute-start | bytes 196616 | tf_op jit(solution)/shard_map/ppermute | solution.py:289
  15.1 7.1 %collective-permute-start.5 = (bf16[32,1024]{1,0:T(8,128)(2,1)S(1)}, bf16[32,1024]{1,0:T(8,128)(2,1)S(1)}, u32[]{:S(2)}, u32[]{:S(2)}) collective-permute-start(bf16[32,1024]{1,0:T(8,128)(2,1)S(1)} %get-tuple-element.28), channel_id=1, source_target_pairs={{0,14},{1,15},{2,12},{3,13},{4,10},{5,11},{6,8},{7,9},{8,6},{9,7},... | collective-permute-start | bytes 196616 | tf_op jit(solution)/shard_map/ppermute | solution.py:289
  17.4 5.0 %collective-permute-start.6 = (bf16[32,1024]{1,0:T(8,128)(2,1)S(1)}, bf16[32,1024]{1,0:T(8,128)(2,1)S(1)}, u32[]{:S(2)}, u32[]{:S(2)}) collective-permute-start(bf16[32,1024]{1,0:T(8,128)(2,1)S(1)} %get-tuple-element.29), channel_id=1, source_target_pairs={{0,4},{1,5},{2,6},{3,7},{4,0},{5,1},{6,2},{7,3},{8,12},{9,13},{10,... | collective-permute-start | bytes 196616 | tf_op jit(solution)/shard_map/ppermute | solution.py:289
  18.4 4.5 %collective-permute-start.7 = (bf16[32,1024]{1,0:T(8,128)(2,1)S(1)}, bf16[32,1024]{1,0:T(8,128)(2,1)S(1)}, u32[]{:S(2)}, u32[]{:S(2)}) collective-permute-start(bf16[32,1024]{1,0:T(8,128)(2,1)S(1)} %get-tuple-element.30), channel_id=1, source_target_pairs={{0,2},{1,3},{2,0},{3,1},{4,6},{5,7},{6,4},{7,5},{8,10},{9,11},{10,... | collective-permute-start | bytes 196616 | tf_op jit(solution)/shard_map/ppermute | solution.py:289
where the time goes:
time: 24.6 us; the launch traced here: 24.3 us
  starting transfers between devices  13.9 us (57%)
  Pallas kernels  6.38 us (26%)
  waiting for transfers between devices  3.94 us (16%)
    ppermute x7, starting transfers between devices, local(): lax.ppermute(part, 'chan', [(i, partner(i // CORES, distance) * CORES + i...  13.4 us
    pallas_call x1, Pallas kernels, local(): pl.pallas_call(rows_kernel, out_shape=[pltpu.VMEM((chips * count, samples...  4.07 us
    ppermute x7, waiting for transfers between devices, local(): lax.ppermute(part, 'chan', [(i, partner(i // CORES, distance) * CORES + i...  2.77 us
    pallas_call x1, Pallas kernels, local(): pl.pallas_call(scores_kernel, out_shape=jax.ShapeDtypeStruct((trials, tem...  1.38 us
    ppermute x1, waiting for transfers between devices, local(): got = lax.ppermute(give, 'chan', [(i, i ^ 1) for i in devices])  1.16 us
    pallas_call x1, Pallas kernels, local(): pl.pallas_call(functools.partial(tables_kernel, bands=bands), out_shape=(...  0.9 us
    ppermute x1, starting transfers between devices, local(): got = lax.ppermute(give, 'chan', [(i, i ^ 1) for i in devices])  0.55 us
  transfers between devices with their start and end apart: 8, of which 5 were waited for; matrix products, arithmetic and copies ran while one was open for 0% of the time, Pallas kernels for 4%

commit v1 on v0

--- a/solution.py
+++ b/solution.py
@@ -15,6 +15,7 @@
 BLOCK = 128
 FINE = 8
 COARSE = MAXD // FINE
+PAIRED = 2
 TILE = 256
 HALF = 16
 CORES = 2
@@ -41,7 +42,7 @@
 
 def rows_kernel(
     spectra_hbm, delay_hbm, base_hbm, keep_ref, give_ref,
-    spectra_ref, delay_ref, base_ref, tables_ref, terms_ref, sums_ref, rows_ref, sems,
+    spectra_ref, delay_ref, base_ref, moves_ref, tables_ref, terms_ref, sums_ref, rows_ref, sems,
 ):
     me = lax.axis_index("chan")
     chip, core = me // CORES, me % CORES
@@ -59,12 +60,41 @@
         large.append(pltpu.make_async_copy(spectra_hbm.at[part], spectra_ref.at[part], sems.at[band]))
     delays = pltpu.make_async_copy(delay_hbm, delay_ref, sems.at[bands])
     bases = pltpu.make_async_copy(base_hbm, base_ref, sems.at[bands + 1])
+    delays.start()
     large[0].start()
-    delays.start()
     for copy in large[1:]:
         copy.start()
     bases.start()
     rows_ref[:, bands * NDELAY :, :] = jnp.zeros((blocks, rows_ref.shape[1] - bands * NDELAY, BLOCK), jnp.float32)
+
+    row = lax.broadcasted_iota(jnp.int32, (2 * BLOCK, 2 * BLOCK), 0)
+    lane = lax.broadcasted_iota(jnp.int32, (2 * BLOCK, 2 * BLOCK), 1)
+    for pair in range(PAIRED // 2):
+        fine = FINE - PAIRED + 2 * pair + lane // BLOCK
+        move = jnp.where(row == BLOCK + lane % BLOCK - fine, 1.0, 0.0)
+        moves_ref[:, pair * 2 * BLOCK : (pair + 1) * 2 * BLOCK] = move.astype(jnp.bfloat16)
+
+    def move_pair(band, pair):
+        slot = band % 2
+        pieces = []
+        for block in range(blocks):
+            for start in (0, depth):
+                now = terms_ref[slot, start : start + SUB_CH, block * BLOCK : (block + 1) * BLOCK]
+                if block:
+                    earlier = terms_ref[slot, start : start + SUB_CH, (block - 1) * BLOCK : block * BLOCK]
+                else:
+                    earlier = jnp.zeros_like(now)
+                pieces.append(jnp.concatenate([earlier, now], axis=1))
+        moved = jnp.dot(
+            jnp.concatenate(pieces, axis=0), moves_ref[:, pair * 2 * BLOCK : (pair + 1) * 2 * BLOCK], preferred_element_type=jnp.float32
+        ).astype(jnp.bfloat16)
+        for block in range(blocks):
+            for term, start in enumerate((0, depth)):
+                rows = slice((2 * block + term) * SUB_CH, (2 * block + term + 1) * SUB_CH)
+                for side in range(2):
+                    at = start + (FINE - PAIRED + 2 * pair + side) * SUB_CH
+                    piece = moved[rows, side * BLOCK : (side + 1) * BLOCK]
+                    terms_ref[slot, at : at + SUB_CH, block * BLOCK : (block + 1) * BLOCK] = piece
 
     def tabulate(band):
         lane = lax.broadcasted_iota(jnp.int32, (NDELAY, channels), 1)
@@ -102,15 +132,18 @@
 
     def drain(band, start):
         slot = band % 2
-        total = sums_ref[slot, start : start + HALF, :]
+        total = sums_ref[slot, start : start + 8, :]
         for coarse in range(1, COARSE):
             at = coarse * NDELAY + start
-            total = total + later(sums_ref[slot, at : at + HALF, :], coarse * FINE)
+            total = total + later(sums_ref[slot, at : at + 8, :], coarse * FINE)
         total = total * SUB_CH ** (-0.5)
         for block in range(blocks):
             at = band * NDELAY + start
-            rows_ref[block, at : at + HALF, :] = total[:, block * BLOCK : (block + 1) * BLOCK]
-
+            rows_ref[block, at : at + 8, :] = total[:, block * BLOCK : (block + 1) * BLOCK]
+
+    delays.wait()
+    for band in range(bands):
+        tabulate(band)
     tiles = samples // TILE
     for step in range(bands + 2):
         if step < bands:
@@ -118,17 +151,16 @@
         for tile in range(tiles):
             if step < bands:
                 for fine in range(tile * FINE // tiles, (tile + 1) * FINE // tiles):
-                    fill(step, fine)
+                    if fine < FINE - PAIRED:
+                        fill(step, fine)
+                    elif (fine - FINE + PAIRED) % 2 == 0:
+                        move_pair(step, (fine - FINE + PAIRED) // 2)
             if 1 <= step <= bands:
                 multiply(step - 1, tile)
             if step >= 2:
-                for start in range(0, NDELAY, HALF):
-                    if (start // HALF + 1) * tiles // (NDELAY // HALF) - 1 == tile:
+                for start in range(0, NDELAY, 8):
+                    if (start // 8 + 1) * tiles // (NDELAY // 8) - 1 == tile:
                         drain(step - 2, start)
-        if step < bands:
-            if step == 0:
-                delays.wait()
-            tabulate(step)
 
     bases.wait()
     place = lax.broadcasted_iota(jnp.int32, (2 * SPAN, BLOCK), 0)
@@ -254,6 +286,7 @@
             pltpu.VMEM((channels, samples), jnp.float32),
             pltpu.VMEM((NDELAY, channels), jnp.int32),
             pltpu.SMEM((bands, owners), jnp.int32),
+            pltpu.VMEM((2 * BLOCK, PAIRED * BLOCK), jnp.bfloat16),
             pltpu.VMEM((bands, COARSE * NDELAY, depth), jnp.bfloat16),
             pltpu.VMEM((2, 2 * depth, samples), jnp.bfloat16),
             pltpu.VMEM((2, COARSE * NDELAY, samples), jnp.float32),

time: 24.6 us -> 24.3 us (0.988)
  Pallas kernels: 6.38 us -> 6.04 us
    pallas_call x1, Pallas kernels: 4.07 us -> 3.72 us  [local(): pl.pallas_call(rows_kernel, out_shape=[pltpu.VMEM((chips * count, samples...]
where the time goes in v1:
time: 24.3 us; the launch traced here: 23.9 us
  starting transfers between devices  13.9 us (57%)
  Pallas kernels  6.04 us (25%)
  waiting for transfers between devices  3.95 us (16%)
    ppermute x7, starting transfers between devices, local(): lax.ppermute(part, 'chan', [(i, partner(i // CORES, distance) * CORES + i...  13.4 us
    pallas_call x1, Pallas kernels, local(): pl.pallas_call(rows_kernel, out_shape=[pltpu.VMEM((chips * count, samples...  3.72 us
    ppermute x7, waiting for transfers between devices, local(): lax.ppermute(part, 'chan', [(i, partner(i // CORES, distance) * CORES + i...  2.79 us
    pallas_call x1, Pallas kernels, local(): pl.pallas_call(scores_kernel, out_shape=jax.ShapeDtypeStruct((trials, tem...  1.39 us
    ppermute x1, waiting for transfers between devices, local(): got = lax.ppermute(give, 'chan', [(i, i ^ 1) for i in devices])  1.16 us
    pallas_call x1, Pallas kernels, local(): pl.pallas_call(functools.partial(tables_kernel, bands=bands), out_shape=(...  0.9 us
    ppermute x1, starting transfers between devices, local(): got = lax.ppermute(give, 'chan', [(i, i ^ 1) for i in devices])  0.55 us
  transfers between devices with their start and end apart: 8, of which 5 were waited for; matrix products, arithmetic and copies ran while one was open for 0% of the time, Pallas kernels for 4%

profile of v1, /device:TPU:0, one launch (start us, length us, event | category | flops | bytes accessed | tf_op | source)
XLA Modules:
  0.0 23.9 jit_solution(8863190850232593415)
XLA Ops:
  0.0 3.7 %rows.1 = (bf16[128,1024]{1,0:T(8,128)(2,1)S(1)}, bf16[128,1024]{1,0:T(8,128)(2,1)S(1)}) custom-call(f32[128,1024]{1,0:T(8,128)} %spectra_hbm.1, s32[32,128]{1,0:T(8,128)} %bitcast.4, s32[4,16]{1,0:T(4,128)} %bitcast.5), custom_call_target="tpu_custom_call" | custom-call | tf_op jit(solution)/shard_map/rows/pallas_call | solution.py:281
  3.7 0.6 %collective-permute-start = (bf16[128,1024]{1,0:T(8,128)(2,1)S(1)}, bf16[128,1024]{1,0:T(8,128)(2,1)S(1)}, u32[]{:S(2)}, u32[]{:S(2)}) collective-permute-start(bf16[128,1024]{1,0:T(8,128)(2,1)S(1)} %get-tuple-element.19), channel_id=1, source_target_pairs={{0,1},{1,0},{2,3},{3,2},{4,5},{5,4},{6,7},{7,6},{8,9},{9,8},{10,11... | collective-permute-start | bytes 786440 | tf_op jit(solution)/shard_map/ppermute | solution.py:311
  4.3 1.2 %collective-permute-done.got_ref = bf16[128,1024]{1,0:T(8,128)(2,1)S(1)} collective-permute-done((bf16[128,1024]{1,0:T(8,128)(2,1)S(1)}, bf16[128,1024]{1,0:T(8,128)(2,1)S(1)}, u32[]{:S(2)}, u32[]{:S(2)}) %collective-permute-start) | collective-permute-done | bytes 262176 | tf_op jit(solution)/shard_map/ppermute | solution.py:311
  5.5 4.0 %collective-permute-start.1 = (bf16[32,1024]{1,0:T(8,128)(2,1)S(1)}, bf16[32,1024]{1,0:T(8,128)(2,1)S(1)}, u32[]{:S(2)}, u32[]{:S(2)}) collective-permute-start(bf16[32,1024]{1,0:T(8,128)(2,1)S(1)} %get-tuple-element.24), channel_id=1, source_target_pairs={{0,8},{1,9},{2,10},{3,11},{4,12},{5,13},{6,14},{7,15},{8,0},{9,1},... | collective-permute-start | bytes 196616 | tf_op jit(solution)/shard_map/ppermute | solution.py:322
  9.5 1.3 %collective-permute-start.2 = (bf16[32,1024]{1,0:T(8,128)(2,1)S(1)}, bf16[32,1024]{1,0:T(8,128)(2,1)S(1)}, u32[]{:S(2)}, u32[]{:S(2)}) collective-permute-start(bf16[32,1024]{1,0:T(8,128)(2,1)S(1)} %get-tuple-element.25), channel_id=1, source_target_pairs={{0,10},{1,11},{2,8},{3,9},{4,14},{5,15},{6,12},{7,13},{8,2},{9,3},... | collective-permute-start | bytes 196616 | tf_op jit(solution)/shard_map/ppermute | solution.py:322
  10.8 1.5 %collective-permute-start.3 = (bf16[32,1024]{1,0:T(8,128)(2,1)S(1)}, bf16[32,1024]{1,0:T(8,128)(2,1)S(1)}, u32[]{:S(2)}, u32[]{:S(2)}) collective-permute-start(bf16[32,1024]{1,0:T(8,128)(2,1)S(1)} %get-tuple-element.26), channel_id=1, source_target_pairs={{0,6},{1,7},{2,4},{3,5},{4,2},{5,3},{6,0},{7,1},{8,14},{9,15},{10,... | collective-permute-start | bytes 196616 | tf_op jit(solution)/shard_map/ppermute | solution.py:322
  12.3 2.5 %collective-permute-start.4 = (bf16[32,1024]{1,0:T(8,128)(2,1)S(1)}, bf16[32,1024]{1,0:T(8,128)(2,1)S(1)}, u32[]{:S(2)}, u32[]{:S(2)}) collective-permute-start(bf16[32,1024]{1,0:T(8,128)(2,1)S(1)} %get-tuple-element.27), channel_id=1, source_target_pairs={{0,12},{1,13},{2,14},{3,15},{4,8},{5,9},{6,10},{7,11},{8,4},{9,5},... | collective-permute-start | bytes 196616 | tf_op jit(solution)/shard_map/ppermute | solution.py:322
  14.8 2.3 %collective-permute-start.5 = (bf16[32,1024]{1,0:T(8,128)(2,1)S(1)}, bf16[32,1024]{1,0:T(8,128)(2,1)S(1)}, u32[]{:S(2)}, u32[]{:S(2)}) collective-permute-start(bf16[32,1024]{1,0:T(8,128)(2,1)S(1)} %get-tuple-element.28), channel_id=1, source_target_pairs={{0,14},{1,15},{2,12},{3,13},{4,10},{5,11},{6,8},{7,9},{8,6},{9,7},... | collective-permute-start | bytes 196616 | tf_op jit(solution)/shard_map/ppermute | solution.py:322
  17.1 0.0 collective-permute-done.1.rest_0_
  17.1 0.0 collective-permute-start.6
  17.1 0.9 %collective-permute-done.2.rest_1_ = bf16[32,1024]{1,0:T(8,128)(2,1)S(1)} collective-permute-done((bf16[32,1024]{1,0:T(8,128)(2,1)S(1)}, bf16[32,1024]{1,0:T(8,128)(2,1)S(1)}, u32[]{:S(2)}, u32[]{:S(2)}) %collective-permute-start.2) | collective-permute-done | bytes 65568 | tf_op jit(solution)/shard_map/ppermute | solution.py:322
  18.0 1.8 %collective-permute-start.7 = (bf16[32,1024]{1,0:T(8,128)(2,1)S(1)}, bf16[32,1024]{1,0:T(8,128)(2,1)S(1)}, u32[]{:S(2)}, u32[]{:S(2)}) collective-permute-start(bf16[32,1024]{1,0:T(8,128)(2,1)S(1)} %get-tuple-element.30), channel_id=1, source_target_pairs={{0,2},{1,3},{2,0},{3,1},{4,6},{5,7},{6,4},{7,5},{8,10},{9,11},{10,... | collective-permute-start | bytes 196616 | tf_op jit(solution)/shard_map/ppermute | solution.py:322
  19.8 0.9 %tables.1 = (bf16[16,256]{1,0:T(8,128)(2,1)S(1)}, s32[16,128]{1,0:T(8,128)S(1)}, s32[8,128]{1,0:T(8,128)S(1)}, bf16[384,256]{1,0:T(8,128)(2,1)S(1)}) custom-call(s32[16,64]{1,0:T(8,128)} %offset_ref.1, s32[1,16]{1,0:T(1,128)} %bitcast.6, s32[1,8]{1,0:T(1,128)} %bitcast.7), custom_call_target="tpu_custom_call" | custom-call | tf_op jit(solution)/shard_map/tables/pallas_call | solution.py:299
  20.7 0.0 collective-permute-done.3.rest_2_
  20.7 0.0 collective-permute-done.4.rest_3_
  20.7 1.2 %collective-permute-done.5.rest_4_ = bf16[32,1024]{1,0:T(8,128)(2,1)S(1)} collective-permute-done((bf16[32,1024]{1,0:T(8,128)(2,1)S(1)}, bf16[32,1024]{1,0:T(8,128)(2,1)S(1)}, u32[]{:S(2)}, u32[]{:S(2)}) %collective-permute-start.5) | collective-permute-done | bytes 65568 | tf_op jit(solution)/shard_map/ppermute | solution.py:322
  21.9 0.2 collective-permute-done.6.rest_5_
  22.1 0.5 %collective-permute-done.7.rest_6_ = bf16[32,1024]{1,0:T(8,128)(2,1)S(1)} collective-permute-done((bf16[32,1024]{1,0:T(8,128)(2,1)S(1)}, bf16[32,1024]{1,0:T(8,128)(2,1)S(1)}, u32[]{:S(2)}, u32[]{:S(2)}) %collective-permute-start.7) | collective-permute-done | bytes 65568 | tf_op jit(solution)/shard_map/ppermute | solution.py:322
  22.6 1.4 %scores.1 = f32[16,8,1024]{2,1,0:T(8,128)} custom-call(bf16[128,1024]{1,0:T(8,128)(2,1)S(1)} %get-tuple-element.18.keep_ref, bf16[128,1024]{1,0:T(8,128)(2,1)S(1)} %collective-permute-done.got_ref, bf16[16,256]{1,0:T(8,128)(2,1)S(1)} %get-tuple-element.20.picker_ref, s32[16,128]{1,0:T(8,128)S(1)} %get-tuple-element.21.shift_ref, ...), custom_call_target="tpu_custom_call" | custom-call | tf_op jit(solution)/shard_map/scores/pallas_call | solution.py:324
  (1 shorter events, 0.0 us)
Async XLA Ops:
  3.7 1.7 %collective-permute-start = (bf16[128,1024]{1,0:T(8,128)(2,1)S(1)}, bf16[128,1024]{1,0:T(8,128)(2,1)S(1)}, u32[]{:S(2)}, u32[]{:S(2)}) collective-permute-start(bf16[128,1024]{1,0:T(8,128)(2,1)S(1)} %get-tuple-element.19), channel_id=1, source_target_pairs={{0,1},{1,0},{2,3},{3,2},{4,5},{5,4},{6,7},{7,6},{8,9},{9,8},{10,11... | collective-permute-start | bytes 786440 | tf_op jit(solution)/shard_map/ppermute | solution.py:311
  5.5 11.6 %collective-permute-start.1 = (bf16[32,1024]{1,0:T(8,128)(2,1)S(1)}, bf16[32,1024]{1,0:T(8,128)(2,1)S(1)}, u32[]{:S(2)}, u32[]{:S(2)}) collective-permute-start(bf16[32,1024]{1,0:T(8,128)(2,1)S(1)} %get-tuple-element.24), channel_id=1, source_target_pairs={{0,8},{1,9},{2,10},{3,11},{4,12},{5,13},{6,14},{7,15},{8,0},{9,1},... | collective-permute-start | bytes 196616 | tf_op jit(solution)/shard_map/ppermute | solution.py:322
  9.5 8.5 %collective-permute-start.2 = (bf16[32,1024]{1,0:T(8,128)(2,1)S(1)}, bf16[32,1024]{1,0:T(8,128)(2,1)S(1)}, u32[]{:S(2)}, u32[]{:S(2)}) collective-permute-start(bf16[32,1024]{1,0:T(8,128)(2,1)S(1)} %get-tuple-element.25), channel_id=1, source_target_pairs={{0,10},{1,11},{2,8},{3,9},{4,14},{5,15},{6,12},{7,13},{8,2},{9,3},... | collective-permute-start | bytes 196616 | tf_op jit(solution)/shard_map/ppermute | solution.py:322
  10.8 9.9 %collective-permute-start.3 = (bf16[32,1024]{1,0:T(8,128)(2,1)S(1)}, bf16[32,1024]{1,0:T(8,128)(2,1)S(1)}, u32[]{:S(2)}, u32[]{:S(2)}) collective-permute-start(bf16[32,1024]{1,0:T(8,128)(2,1)S(1)} %get-tuple-element.26), channel_id=1, source_target_pairs={{0,6},{1,7},{2,4},{3,5},{4,2},{5,3},{6,0},{7,1},{8,14},{9,15},{10,... | collective-permute-start | bytes 196616 | tf_op jit(solution)/shard_map/ppermute | solution.py:322
  12.3 8.4 %collective-permute-start.4 = (bf16[32,1024]{1,0:T(8,128)(2,1)S(1)}, bf16[32,1024]{1,0:T(8,128)(2,1)S(1)}, u32[]{:S(2)}, u32[]{:S(2)}) collective-permute-start(bf16[32,1024]{1,0:T(8,128)(2,1)S(1)} %get-tuple-element.27), channel_id=1, source_target_pairs={{0,12},{1,13},{2,14},{3,15},{4,8},{5,9},{6,10},{7,11},{8,4},{9,5},... | collective-permute-start | bytes 196616 | tf_op jit(solution)/shard_map/ppermute | solution.py:322
  14.8 7.1 %collective-permute-start.5 = (bf16[32,1024]{1,0:T(8,128)(2,1)S(1)}, bf16[32,1024]{1,0:T(8,128)(2,1)S(1)}, u32[]{:S(2)}, u32[]{:S(2)}) collective-permute-start(bf16[32,1024]{1,0:T(8,128)(2,1)S(1)} %get-tuple-element.28), channel_id=1, source_target_pairs={{0,14},{1,15},{2,12},{3,13},{4,10},{5,11},{6,8},{7,9},{8,6},{9,7},... | collective-permute-start | bytes 196616 | tf_op jit(solution)/shard_map/ppermute | solution.py:322
  17.1 5.0 %collective-permute-start.6 = (bf16[32,1024]{1,0:T(8,128)(2,1)S(1)}, bf16[32,1024]{1,0:T(8,128)(2,1)S(1)}, u32[]{:S(2)}, u32[]{:S(2)}) collective-permute-start(bf16[32,1024]{1,0:T(8,128)(2,1)S(1)} %get-tuple-element.29), channel_id=1, source_target_pairs={{0,4},{1,5},{2,6},{3,7},{4,0},{5,1},{6,2},{7,3},{8,12},{9,13},{10,... | collective-permute-start | bytes 196616 | tf_op jit(solution)/shard_map/ppermute | solution.py:322
  18.0 4.5 %collective-permute-start.7 = (bf16[32,1024]{1,0:T(8,128)(2,1)S(1)}, bf16[32,1024]{1,0:T(8,128)(2,1)S(1)}, u32[]{:S(2)}, u32[]{:S(2)}) collective-permute-start(bf16[32,1024]{1,0:T(8,128)(2,1)S(1)} %get-tuple-element.30), channel_id=1, source_target_pairs={{0,2},{1,3},{2,0},{3,1},{4,6},{5,7},{6,4},{7,5},{8,10},{9,11},{10,... | collective-permute-start | bytes 196616 | tf_op jit(solution)/shard_map/ppermute | solution.py:322

commit v2 on v1

--- a/solution.py
+++ b/solution.py
@@ -19,7 +19,7 @@
 TILE = 256
 HALF = 16
 CORES = 2
-ORDER = (4, 5, 3, 6, 7, 2, 1)
+ORDER = (4, 5, 3, 7, 6, 2, 1)
 
 
 def later(x, amount):
@@ -41,17 +41,12 @@
 
 
 def rows_kernel(
-    spectra_hbm, delay_hbm, base_hbm, keep_ref, give_ref,
-    spectra_ref, delay_ref, base_ref, moves_ref, tables_ref, terms_ref, sums_ref, rows_ref, sems,
+    spectra_hbm, delay_hbm, base_hbm, rows_ref, give_ref,
+    spectra_ref, delay_ref, base_ref, moves_ref, tables_ref, terms_ref, sums_ref, sems,
 ):
-    me = lax.axis_index("chan")
-    chip, core = me // CORES, me % CORES
     channels, samples = spectra_ref.shape
     bands = channels // SUB_CH
-    owners = base_ref.shape[1]
     depth = FINE * SUB_CH
-    count = bands * SPAN
-    chips = owners // CORES
     blocks = samples // BLOCK
 
     large = []
@@ -163,19 +158,33 @@
                         drain(step - 2, start)
 
     bases.wait()
+    pick_windows(rows_ref, base_ref, give_ref, 1)
+
+
+def pick_windows(rows_ref, base_ref, target, side):
+    me = lax.axis_index("chan")
+    chip, core = me // CORES, me % CORES
+    bands, owners = base_ref.shape
+    count = bands * SPAN
     place = lax.broadcasted_iota(jnp.int32, (2 * SPAN, BLOCK), 0)
-    for side, target in ((1, give_ref), (0, keep_ref)):
-        for distance in range(chips):
-            owner = partner(chip, distance) * CORES + (core + side) % CORES
-            begins = [band * NDELAY + base_ref[band, owner] for band in range(bands)]
-            for block in range(blocks):
-                pairs = []
-                for band in range(0, bands, 2):
-                    upper = rows_ref[block, pl.ds(begins[band], 2 * SPAN), :]
-                    lower = rows_ref[block, pl.ds(begins[band + 1] - SPAN, 2 * SPAN), :]
-                    pairs.append(jnp.where(place < SPAN, upper, lower))
-                picked = jnp.concatenate(pairs, axis=0).astype(jnp.bfloat16)
-                target[distance * count : (distance + 1) * count, block * BLOCK : (block + 1) * BLOCK] = picked
+    for distance in range(owners // CORES):
+        owner = partner(chip, distance) * CORES + (core + side) % CORES
+        begins = [band * NDELAY + base_ref[band, owner] for band in range(bands)]
+        for block in range(rows_ref.shape[0]):
+            pairs = []
+            for band in range(0, bands, 2):
+                upper = rows_ref[block, pl.ds(begins[band], 2 * SPAN), :]
+                lower = rows_ref[block, pl.ds(begins[band + 1] - SPAN, 2 * SPAN), :]
+                pairs.append(jnp.where(place < SPAN, upper, lower))
+            picked = jnp.concatenate(pairs, axis=0).astype(jnp.bfloat16)
+            target[distance * count : (distance + 1) * count, block * BLOCK : (block + 1) * BLOCK] = picked
+
+
+def keep_kernel(rows_ref, base_hbm, keep_ref, base_ref, sem):
+    copy = pltpu.make_async_copy(base_hbm, base_ref, sem)
+    copy.start()
+    copy.wait()
+    pick_windows(rows_ref, base_ref, keep_ref, 0)
 
 
 def tables_kernel(offset_ref, shift_in, length_in, picker_ref, shift_ref, length_ref, ones_ref, *, bands):
@@ -278,9 +287,12 @@
         pltpu.with_memory_space_constraint(array, pltpu.HBM)
         for array in (spectra, chan_delay.T, window_base.T, trial_offset, shift_blocks.reshape(1, trials), template_len.reshape(1, templates))
     ]
-    keep, give = pl.pallas_call(
+    rows, give = pl.pallas_call(
         rows_kernel,
-        out_shape=[pltpu.VMEM((chips * count, samples), jnp.bfloat16)] * 2,
+        out_shape=(
+            pltpu.VMEM((samples // BLOCK, bands * NDELAY + 2 * SPAN, BLOCK), jnp.float32),
+            pltpu.VMEM((chips * count, samples), jnp.bfloat16),
+        ),
         in_specs=[anywhere] * 3,
         scratch_shapes=[
             pltpu.VMEM((channels, samples), jnp.float32),
@@ -290,7 +302,6 @@
             pltpu.VMEM((bands, COARSE * NDELAY, depth), jnp.bfloat16),
             pltpu.VMEM((2, 2 * depth, samples), jnp.bfloat16),
             pltpu.VMEM((2, COARSE * NDELAY, samples), jnp.float32),
-            pltpu.VMEM((samples // BLOCK, bands * NDELAY + 2 * SPAN, BLOCK), jnp.float32),
             pltpu.SemaphoreType.DMA((bands + 2,)),
         ],
         compiler_params=limits,
@@ -309,6 +320,14 @@
     )(*arrays[3:])
     devices = range(owners)
     got = lax.ppermute(give, "chan", [(i, i ^ 1) for i in devices])
+    keep = pl.pallas_call(
+        keep_kernel,
+        out_shape=pltpu.VMEM((chips * count, samples), jnp.bfloat16),
+        in_specs=[inside, anywhere],
+        scratch_shapes=[pltpu.SMEM((bands, owners), jnp.int32), pltpu.SemaphoreType.DMA],
+        compiler_params=limits,
+        name="keep",
+    )(rows, arrays[2])
     got = pltpu.with_memory_space_constraint(got, pltpu.VMEM)
     parts = pl.pallas_call(
         join_kernel,

time: 24.3 us -> 24.3 us (level)
  the two profiles are of different devices: /device:TPU:0 before, /device:TPU:26 now
where the time goes in v2:
time: 24.3 us; the launch traced here: 24 us
  starting transfers between devices  9.19 us (38%)
  waiting for transfers between devices  8.02 us (33%)
  Pallas kernels  6.78 us (28%)
    ppermute x7, starting transfers between devices, local(): lax.ppermute(part, 'chan', [(i, partner(i // CORES, distance) * CORES + i...  9.12 us
    ppermute x7, waiting for transfers between devices, local(): lax.ppermute(part, 'chan', [(i, partner(i // CORES, distance) * CORES + i...  7.31 us
    pallas_call x1, Pallas kernels, local(): pl.pallas_call(rows_kernel, out_shape=(pltpu.VMEM((samples // BLOCK, band...  3.65 us
    pallas_call x1, Pallas kernels, local(): pl.pallas_call(scores_kernel, out_shape=jax.ShapeDtypeStruct((trials, tem...  1.39 us
    pallas_call x1, Pallas kernels, local(): pl.pallas_call(functools.partial(tables_kernel, bands=bands), out_shape=(...  0.9 us
    pallas_call x1, Pallas kernels, local(): pl.pallas_call(keep_kernel, out_shape=pltpu.VMEM((chips * count, samples)...  0.81 us
    ppermute x1, waiting for transfers between devices, local(): got = lax.ppermute(give, 'chan', [(i, i ^ 1) for i in devices])  0.71 us
  transfers between devices with their start and end apart: 8, of which 4 were waited for; matrix products, arithmetic and copies ran while one was open for 0% of the time, Pallas kernels for 7%

profile of v2, /device:TPU:26, one launch (start us, length us, event | category | flops | bytes accessed | tf_op | source)
XLA Modules:
  0.0 24.0 jit_solution(14582774758884509852)
XLA Ops:
  0.0 3.7 %rows.1 = (f32[8,136,128]{2,1,0:T(8,128)S(1)}, bf16[128,1024]{1,0:T(8,128)(2,1)S(1)}) custom-call(f32[128,1024]{1,0:T(8,128)} %spectra_hbm.1, s32[32,128]{1,0:T(8,128)} %bitcast.4, s32[4,16]{1,0:T(4,128)} %bitcast.5), custom_call_target="tpu_custom_call" | custom-call | tf_op jit(solution)/shard_map/rows/pallas_call | solution.py:290
  3.7 0.1 collective-permute-start
  3.7 0.8 %keep.1.keep_ref = bf16[128,1024]{1,0:T(8,128)(2,1)S(1)} custom-call(f32[8,136,128]{2,1,0:T(8,128)S(1)} %get-tuple-element.18.rows_ref, s32[4,16]{1,0:T(4,128)} %bitcast.6), custom_call_target="tpu_custom_call" | custom-call | tf_op jit(solution)/shard_map/keep/pallas_call | solution.py:323
  4.6 0.7 %collective-permute-done.got_ref = bf16[128,1024]{1,0:T(8,128)(2,1)S(1)} collective-permute-done((bf16[128,1024]{1,0:T(8,128)(2,1)S(1)}, bf16[128,1024]{1,0:T(8,128)(2,1)S(1)}, u32[]{:S(2)}, u32[]{:S(2)}) %collective-permute-start) | collective-permute-done | bytes 262176 | tf_op jit(solution)/shard_map/ppermute | solution.py:322
  5.3 0.4 %collective-permute-start.1 = (bf16[32,1024]{1,0:T(8,128)(2,1)S(1)}, bf16[32,1024]{1,0:T(8,128)(2,1)S(1)}, u32[]{:S(2)}, u32[]{:S(2)}) collective-permute-start(bf16[32,1024]{1,0:T(8,128)(2,1)S(1)} %get-tuple-element.24), channel_id=1, source_target_pairs={{0,8},{1,9},{2,10},{3,11},{4,12},{5,13},{6,14},{7,15},{8,0},{9,1},... | collective-permute-start | bytes 196616 | tf_op jit(solution)/shard_map/ppermute | solution.py:341
  5.7 3.5 %collective-permute-start.2 = (bf16[32,1024]{1,0:T(8,128)(2,1)S(1)}, bf16[32,1024]{1,0:T(8,128)(2,1)S(1)}, u32[]{:S(2)}, u32[]{:S(2)}) collective-permute-start(bf16[32,1024]{1,0:T(8,128)(2,1)S(1)} %get-tuple-element.25), channel_id=1, source_target_pairs={{0,10},{1,11},{2,8},{3,9},{4,14},{5,15},{6,12},{7,13},{8,2},{9,3},... | collective-permute-start | bytes 196616 | tf_op jit(solution)/shard_map/ppermute | solution.py:341
  9.2 0.4 %collective-permute-start.3 = (bf16[32,1024]{1,0:T(8,128)(2,1)S(1)}, bf16[32,1024]{1,0:T(8,128)(2,1)S(1)}, u32[]{:S(2)}, u32[]{:S(2)}) collective-permute-start(bf16[32,1024]{1,0:T(8,128)(2,1)S(1)} %get-tuple-element.26), channel_id=1, source_target_pairs={{0,6},{1,7},{2,4},{3,5},{4,2},{5,3},{6,0},{7,1},{8,14},{9,15},{10,... | collective-permute-start | bytes 196616 | tf_op jit(solution)/shard_map/ppermute | solution.py:341
  9.6 2.3 %collective-permute-start.4 = (bf16[32,1024]{1,0:T(8,128)(2,1)S(1)}, bf16[32,1024]{1,0:T(8,128)(2,1)S(1)}, u32[]{:S(2)}, u32[]{:S(2)}) collective-permute-start(bf16[32,1024]{1,0:T(8,128)(2,1)S(1)} %get-tuple-element.27), channel_id=1, source_target_pairs={{0,14},{1,15},{2,12},{3,13},{4,10},{5,11},{6,8},{7,9},{8,6},{9,7},... | collective-permute-start | bytes 196616 | tf_op jit(solution)/shard_map/ppermute | solution.py:341
  11.9 2.5 %collective-permute-start.5 = (bf16[32,1024]{1,0:T(8,128)(2,1)S(1)}, bf16[32,1024]{1,0:T(8,128)(2,1)S(1)}, u32[]{:S(2)}, u32[]{:S(2)}) collective-permute-start(bf16[32,1024]{1,0:T(8,128)(2,1)S(1)} %get-tuple-element.28), channel_id=1, source_target_pairs={{0,12},{1,13},{2,14},{3,15},{4,8},{5,9},{6,10},{7,11},{8,4},{9,5},... | collective-permute-start | bytes 196616 | tf_op jit(solution)/shard_map/ppermute | solution.py:341
  14.4 0.0 collective-permute-done.1.rest_0_
  14.4 0.0 collective-permute-start.6
  14.4 4.0 %collective-permute-done.2.rest_1_ = bf16[32,1024]{1,0:T(8,128)(2,1)S(1)} collective-permute-done((bf16[32,1024]{1,0:T(8,128)(2,1)S(1)}, bf16[32,1024]{1,0:T(8,128)(2,1)S(1)}, u32[]{:S(2)}, u32[]{:S(2)}) %collective-permute-start.2) | collective-permute-done | bytes 65568 | tf_op jit(solution)/shard_map/ppermute | solution.py:341
  18.4 0.0 collective-permute-start.7
  18.4 0.9 %tables.1 = (bf16[16,256]{1,0:T(8,128)(2,1)S(1)}, s32[16,128]{1,0:T(8,128)S(1)}, s32[8,128]{1,0:T(8,128)S(1)}, bf16[384,256]{1,0:T(8,128)(2,1)S(1)}) custom-call(s32[16,64]{1,0:T(8,128)} %offset_ref.1, s32[1,16]{1,0:T(1,128)} %bitcast.7, s32[1,8]{1,0:T(1,128)} %bitcast.8), custom_call_target="tpu_custom_call" | custom-call | tf_op jit(solution)/shard_map/tables/pallas_call | solution.py:310
  19.3 0.5 %collective-permute-done.3.rest_2_ = bf16[32,1024]{1,0:T(8,128)(2,1)S(1)} collective-permute-done((bf16[32,1024]{1,0:T(8,128)(2,1)S(1)}, bf16[32,1024]{1,0:T(8,128)(2,1)S(1)}, u32[]{:S(2)}, u32[]{:S(2)}) %collective-permute-start.3) | collective-permute-done | bytes 65568 | tf_op jit(solution)/shard_map/ppermute | solution.py:341
  19.8 0.0 collective-permute-done.4.rest_3_
  19.8 0.0 collective-permute-done.5.rest_4_
  19.8 0.0 collective-permute-done.6.rest_5_
  19.8 2.9 %collective-permute-done.7.rest_6_ = bf16[32,1024]{1,0:T(8,128)(2,1)S(1)} collective-permute-done((bf16[32,1024]{1,0:T(8,128)(2,1)S(1)}, bf16[32,1024]{1,0:T(8,128)(2,1)S(1)}, u32[]{:S(2)}, u32[]{:S(2)}) %collective-permute-start.7) | collective-permute-done | bytes 65568 | tf_op jit(solution)/shard_map/ppermute | solution.py:341
  22.6 1.4 %scores.1 = f32[16,8,1024]{2,1,0:T(8,128)} custom-call(bf16[128,1024]{1,0:T(8,128)(2,1)S(1)} %keep.1.keep_ref, bf16[128,1024]{1,0:T(8,128)(2,1)S(1)} %collective-permute-done.got_ref, bf16[16,256]{1,0:T(8,128)(2,1)S(1)} %get-tuple-element.20.picker_ref, s32[16,128]{1,0:T(8,128)S(1)} %get-tuple-element.21.shift_ref, ...), custom_call_target="tpu_custom_call" | custom-call | tf_op jit(solution)/shard_map/scores/pallas_call | solution.py:343
  (1 shorter events, 0.0 us)
Async XLA Ops:
  3.7 1.6 %collective-permute-start = (bf16[128,1024]{1,0:T(8,128)(2,1)S(1)}, bf16[128,1024]{1,0:T(8,128)(2,1)S(1)}, u32[]{:S(2)}, u32[]{:S(2)}) collective-permute-start(bf16[128,1024]{1,0:T(8,128)(2,1)S(1)} %get-tuple-element.19), channel_id=1, source_target_pairs={{0,1},{1,0},{2,3},{3,2},{4,5},{5,4},{6,7},{7,6},{8,9},{9,8},{10,11... | collective-permute-start | bytes 786440 | tf_op jit(solution)/shard_map/ppermute | solution.py:322
  5.3 9.1 %collective-permute-start.1 = (bf16[32,1024]{1,0:T(8,128)(2,1)S(1)}, bf16[32,1024]{1,0:T(8,128)(2,1)S(1)}, u32[]{:S(2)}, u32[]{:S(2)}) collective-permute-start(bf16[32,1024]{1,0:T(8,128)(2,1)S(1)} %get-tuple-element.24), channel_id=1, source_target_pairs={{0,8},{1,9},{2,10},{3,11},{4,12},{5,13},{6,14},{7,15},{8,0},{9,1},... | collective-permute-start | bytes 196616 | tf_op jit(solution)/shard_map/ppermute | solution.py:341
  5.7 12.7 %collective-permute-start.2 = (bf16[32,1024]{1,0:T(8,128)(2,1)S(1)}, bf16[32,1024]{1,0:T(8,128)(2,1)S(1)}, u32[]{:S(2)}, u32[]{:S(2)}) collective-permute-start(bf16[32,1024]{1,0:T(8,128)(2,1)S(1)} %get-tuple-element.25), channel_id=1, source_target_pairs={{0,10},{1,11},{2,8},{3,9},{4,14},{5,15},{6,12},{7,13},{8,2},{9,3},... | collective-permute-start | bytes 196616 | tf_op jit(solution)/shard_map/ppermute | solution.py:341
  9.2 10.5 %collective-permute-start.3 = (bf16[32,1024]{1,0:T(8,128)(2,1)S(1)}, bf16[32,1024]{1,0:T(8,128)(2,1)S(1)}, u32[]{:S(2)}, u32[]{:S(2)}) collective-permute-start(bf16[32,1024]{1,0:T(8,128)(2,1)S(1)} %get-tuple-element.26), channel_id=1, source_target_pairs={{0,6},{1,7},{2,4},{3,5},{4,2},{5,3},{6,0},{7,1},{8,14},{9,15},{10,... | collective-permute-start | bytes 196616 | tf_op jit(solution)/shard_map/ppermute | solution.py:341
  9.6 10.1 %collective-permute-start.4 = (bf16[32,1024]{1,0:T(8,128)(2,1)S(1)}, bf16[32,1024]{1,0:T(8,128)(2,1)S(1)}, u32[]{:S(2)}, u32[]{:S(2)}) collective-permute-start(bf16[32,1024]{1,0:T(8,128)(2,1)S(1)} %get-tuple-element.27), channel_id=1, source_target_pairs={{0,14},{1,15},{2,12},{3,13},{4,10},{5,11},{6,8},{7,9},{8,6},{9,7},... | collective-permute-start | bytes 196616 | tf_op jit(solution)/shard_map/ppermute | solution.py:341
  11.9 7.8 %collective-permute-start.5 = (bf16[32,1024]{1,0:T(8,128)(2,1)S(1)}, bf16[32,1024]{1,0:T(8,128)(2,1)S(1)}, u32[]{:S(2)}, u32[]{:S(2)}) collective-permute-start(bf16[32,1024]{1,0:T(8,128)(2,1)S(1)} %get-tuple-element.28), channel_id=1, source_target_pairs={{0,12},{1,13},{2,14},{3,15},{4,8},{5,9},{6,10},{7,11},{8,4},{9,5},... | collective-permute-start | bytes 196616 | tf_op jit(solution)/shard_map/ppermute | solution.py:341
  14.4 5.3 %collective-permute-start.6 = (bf16[32,1024]{1,0:T(8,128)(2,1)S(1)}, bf16[32,1024]{1,0:T(8,128)(2,1)S(1)}, u32[]{:S(2)}, u32[]{:S(2)}) collective-permute-start(bf16[32,1024]{1,0:T(8,128)(2,1)S(1)} %get-tuple-element.29), channel_id=1, source_target_pairs={{0,4},{1,5},{2,6},{3,7},{4,0},{5,1},{6,2},{7,3},{8,12},{9,13},{10,... | collective-permute-start | bytes 196616 | tf_op jit(solution)/shard_map/ppermute | solution.py:341
  18.4 4.3 %collective-permute-start.7 = (bf16[32,1024]{1,0:T(8,128)(2,1)S(1)}, bf16[32,1024]{1,0:T(8,128)(2,1)S(1)}, u32[]{:S(2)}, u32[]{:S(2)}) collective-permute-start(bf16[32,1024]{1,0:T(8,128)(2,1)S(1)} %get-tuple-element.30), channel_id=1, source_target_pairs={{0,2},{1,3},{2,0},{3,1},{4,6},{5,7},{6,4},{7,5},{8,10},{9,11},{10,... | collective-permute-start | bytes 196616 | tf_op jit(solution)/shard_map/ppermute | solution.py:341
